TPU v7x, 1024 devices: a whole 4x4x32 slice. The times are simulated.
1024 devices in a mesh: dp: 32 (over x, z_hi, core), expert: 32 (over z_lo, y).
Axes of the slice: x: 4, y: 4, z: 32 (z_hi: 4, z_lo: 8; z = z_hi * 8 + z_lo), core: 2. Of those that a mesh axis runs over, the one named last changes fastest.
Arguments:
- tokens: bfloat16 [131072, 2560], P(('dp', 'expert')), parts along dimension 0, may hold values from -6 to 6
- expert_ids: int32 [131072, 2], P(('dp', 'expert')), parts along dimension 0, may hold values from 0 to 15, all different within a row; in each aligned block of 128 rows (0 to 127, 128 to 255, ...) at most 20 rows name the same one
- gate_weights: float32 [131072, 2], P(('dp', 'expert')), parts along dimension 0, may hold values from 0.1 to 1
- w_gate: bfloat16 [2560, 12288], P(None, 'expert'), may hold values from -0.125 to 0.125
- w_up: bfloat16 [2560, 12288], P(None, 'expert'), may hold values from -0.125 to 0.125
- w_down: bfloat16 [12288, 2560], P('expert'), may hold values from -0.21875 to 0.21875
Outputs:
- moe_out: bfloat16 [131072, 2560], P(('dp', 'expert')), parts along dimension 0
There are 32 independent parts, one for each index of `dp`. A program takes and returns all parts, laid end to end along the dimension named above; an argument that names none is the same for every part. Nothing has to cross between parts.
Inputs may be any that keep to these rules, and one draw needn't show every extreme that they name: `expert_ids`: each row names 2 different experts; in each aligned block of 128 rows (the rows of one device) no expert is named by more than 20 rows, a bound that some block reaches.
All inputs are finite; a program needn't handle non-finite values.
Results may differ from a plain program's by a relative error of at most 0.01.
Values may be sent and summed in bfloat16 or wider, within the bound.
No kernel may reach another device: no remote copies, remote signals or barrier semaphores. Data moves between devices by JAX's collectives and lax.ppermute only.
A program may use at most 64 MiB of HBM per device.

v0:
```python
import jax
import jax.numpy as jnp
from jax import lax
from jax.sharding import PartitionSpec as P

EXPERTS = 16
CAP = 20


def partner(value, axis, stride):
    return lax.ppermute(value, axis, [(i, i ^ 1 << stride) for i in range(lax.axis_size(axis))])


def expert_part(block_rows, gate_cols, up_cols, down_rows):
    gate_act = jnp.dot(block_rows, gate_cols, preferred_element_type=jnp.float32)
    up_act = jnp.dot(block_rows, up_cols, preferred_element_type=jnp.float32)
    hidden = (jax.nn.silu(gate_act) * up_act).astype(jnp.bfloat16)
    return jnp.dot(hidden, down_rows, preferred_element_type=jnp.float32).astype(jnp.bfloat16)


def per_device(tokens, expert_ids, gate_weights, w_gate, w_up, w_down):
    tok_rows, model_width = tokens.shape
    pick_count = expert_ids.shape[1]
    flat_ids = expert_ids.reshape(-1)
    pick_total = flat_ids.shape[0]
    one_hot = (flat_ids[:, None] == jnp.arange(EXPERTS, dtype=jnp.int32)[None, :]).astype(
        jnp.float32
    )
    pick_iota = jnp.arange(pick_total, dtype=jnp.int32)
    lower_tri = (pick_iota[:, None] > pick_iota[None, :]).astype(jnp.float32)
    earlier = jnp.dot(
        lower_tri, one_hot, precision=lax.Precision.HIGHEST, preferred_element_type=jnp.float32
    )
    slot_index = jnp.sum(earlier * one_hot, axis=1).astype(jnp.int32)
    position = flat_ids * CAP + slot_index
    token_of = pick_iota // pick_count
    slot_iota = jnp.arange(EXPERTS * CAP, dtype=jnp.int32)
    pick_slot = (slot_iota[:, None] == position[None, :]).astype(jnp.bfloat16)
    pick_token = (token_of[:, None] == jnp.arange(tok_rows, dtype=jnp.int32)[None, :]).astype(
        jnp.bfloat16
    )
    chooser = jnp.dot(pick_slot, pick_token, preferred_element_type=jnp.float32).astype(
        jnp.bfloat16
    )
    slot_rows = jnp.dot(chooser, tokens, preferred_element_type=jnp.float32).astype(jnp.bfloat16)
    arrived = lax.all_to_all(slot_rows, "expert", split_axis=0, concat_axis=0, tiled=True)
    other_gate, other_up, other_down = partner((w_gate, w_up, w_down), "expert", 0)
    own_part = expert_part(arrived, w_gate, w_up, w_down)
    theirs = expert_part(arrived, other_gate, other_up, other_down)
    expert_out = (own_part.astype(jnp.float32) + theirs.astype(jnp.float32)).astype(jnp.bfloat16)
    returned_rows = lax.all_to_all(expert_out, "expert", split_axis=0, concat_axis=0, tiled=True)
    weighted_picks = pick_token.astype(jnp.float32).T * gate_weights.reshape(-1)[None, :]
    mixer = jnp.dot(
        weighted_picks,
        pick_slot.astype(jnp.float32).T,
        precision=lax.Precision.HIGHEST,
        preferred_element_type=jnp.float32,
    )
    mixed = jnp.dot(
        mixer,
        returned_rows.astype(jnp.float32),
        precision=lax.Precision.HIGHEST,
        preferred_element_type=jnp.float32,
    )
    return mixed.astype(jnp.bfloat16)


def solution(mesh):
    in_specs = (
        P(("dp", "expert"), None),
        P(("dp", "expert"), None),
        P(("dp", "expert"), None),
        P(None, "expert"),
        P(None, "expert"),
        P("expert", None),
    )
    out_specs = P(("dp", "expert"), None)
    return jax.shard_map(
        per_device, mesh=mesh, in_specs=in_specs, out_specs=out_specs, check_vma=False
    )
```

profile of v0, /device:TPU:258, one launch (start us, length us, event | category | flops | bytes accessed | tf_op | source)
XLA Modules:
  0.0 321.7 jit_solution(9095930108070301181)
XLA Ops:
  0.0 0.0 copy-start
  0.0 0.9 copy.8
  0.9 0.1 reshape.31
  1.0 0.2 fusion.5
  1.2 0.0 copy-done
  1.2 0.9 convolution_convert_fusion.2
  2.1 2.2 all_to_all.16
  4.3 15.7 %all-to-all-start = ((bf16[32,10,2560]{2,1,0:T(8,128)(2,1)}), bf16[32,10,2560]{2,1,0:T(8,128)(2,1)}, u32[]{:S(2)}, u32[]{:S(2)}) async-start(bf16[32,10,2560]{2,1,0:T(8,128)(2,1)} %all_to_all.16), calls=%async_computation | async-start | bytes 5242880 | tf_op jit(solution)/shard_map/all_to_all | solution.py:46
  20.0 3.6 %collective-permute-start = (bf16[2560,384]{1,0:T(8,128)(2,1)}, bf16[2560,384]{1,0:T(8,128)(2,1)}, u32[]{:S(2)}, u32[]{:S(2)}) collective-permute-start(bf16[2560,384]{1,0:T(8,128)(2,1)} %param.9), channel_id=1, source_target_pairs={{0,1},{1,0},{2,3},{3,2},{4,5},{5,4},{6,7},{7,6},{8,9},{9,8},{10,11... | collective-permute-start | bytes 5898248 | tf_op jit(solution)/shard_map/ppermute | solution.py:11
  23.6 2.2 collective-permute-start.1
  25.8 3.6 %collective-permute-start.2 = (bf16[384,2560]{1,0:T(8,128)(2,1)}, bf16[384,2560]{1,0:T(8,128)(2,1)}, u32[]{:S(2)}, u32[]{:S(2)}) collective-permute-start(bf16[384,2560]{1,0:T(8,128)(2,1)} %param.11), channel_id=1, source_target_pairs={{0,1},{1,0},{2,3},{3,2},{4,5},{5,4},{6,7},{7,6},{8,9},{9,8},{10,11... | collective-permute-start | bytes 5898248 | tf_op jit(solution)/shard_map/ppermute | solution.py:11
  29.5 108.8 %all-to-all-done = bf16[32,10,2560]{2,1,0:T(8,128)(2,1)} async-done(((bf16[32,10,2560]{2,1,0:T(8,128)(2,1)}), bf16[32,10,2560]{2,1,0:T(8,128)(2,1)}, u32[]{:S(2)}, u32[]{:S(2)}) %all-to-all-start) | async-done | bytes 1638432 | tf_op jit(solution)/shard_map/all_to_all | solution.py:46
  138.2 2.7 all_to_all.18
  141.0 2.5 fusion.30
  143.5 0.0 collective-permute-done
  143.5 2.5 fusion.31
  146.1 5.7 %fusion.3 = f32[320,2560]{1,0:T(8,128)} fusion(bf16[384,2560]{1,0:T(8,128)(2,1)} %param.11, bf16[320,2560]{1,0:T(8,128)(2,1)S(1)} %all_to_all.18, bf16[2560,384]{1,0:T(8,128)(2,1)} %param.10, f32[320,384]{1,0:T(8,128)S(1)} %fusion.30), kind=kOutput, calls=%fused_computation.5 | convolution fusion | flops 1260666880 | bytes 9338880 | tf_op jit(solution)/shard_map/dot_general | solution.py:18
  151.8 0.0 collective-permute-done.1
  151.8 24.6 %collective-permute-done.2 = bf16[384,2560]{1,0:T(8,128)(2,1)} collective-permute-done((bf16[384,2560]{1,0:T(8,128)(2,1)}, bf16[384,2560]{1,0:T(8,128)(2,1)}, u32[]{:S(2)}, u32[]{:S(2)}) %collective-permute-start.2) | collective-permute-done | bytes 1966112 | tf_op jit(solution)/shard_map/ppermute | solution.py:11
  176.5 6.2 %fusion.2 = bf16[320,2560]{1,0:T(8,128)(2,1)} fusion(f32[320,2560]{1,0:T(8,128)} %fusion.3, bf16[384,2560]{1,0:T(8,128)(2,1)} %collective-permute-done.2, f32[320,384]{1,0:T(8,128)S(1)} %fusion.31, bf16[320,2560]{1,0:T(8,128)(2,1)S(1)} %all_to_all.18, bf16[2560,384]{1,0:T(8,128)(2,1)} %collective-permute-done.1), kind=kOutput, calls=%fused_computation.3 | convolution fusion | flops 1262305280 | bytes 10977280 | tf_op jit(solution)/shard_map/dot_general | solution.py:18
  182.7 4.0 %all_to_all.19 = bf16[32,10,2560]{2,1,0:T(8,128)(2,1)} reshape(bf16[320,2560]{1,0:T(8,128)(2,1)} %fusion.2) | data formatting | bytes 3276800 | tf_op jit(solution)/shard_map/all_to_all | solution.py:51
  186.7 0.0 copy-start.1
  186.7 12.1 %all-to-all-start.1 = ((bf16[32,10,2560]{2,1,0:T(8,128)(2,1)}), bf16[32,10,2560]{2,1,0:T(8,128)(2,1)S(1)}, u32[]{:S(2)}, u32[]{:S(2)}) async-start(bf16[32,10,2560]{2,1,0:T(8,128)(2,1)} %all_to_all.19), calls=%async_computation.1 | async-start | bytes 5242880 | tf_op jit(solution)/shard_map/all_to_all | solution.py:51
  198.7 0.0 copy-done.1
  198.7 0.1 copy.7
  198.9 0.1 mul.36
  199.0 0.3 fusion.11
  199.3 116.9 %all-to-all-done.1 = bf16[32,10,2560]{2,1,0:T(8,128)(2,1)S(1)} async-done(((bf16[32,10,2560]{2,1,0:T(8,128)(2,1)}), bf16[32,10,2560]{2,1,0:T(8,128)(2,1)S(1)}, u32[]{:S(2)}, u32[]{:S(2)}) %all-to-all-start.1) | async-done | bytes 1638432 | tf_op jit(solution)/shard_map/all_to_all | solution.py:51
  316.2 2.0 all_to_all.21
  318.2 3.5 %convolution_convert_fusion.3 = bf16[128,2560]{1,0:T(8,128)(2,1)} fusion(f32[128,320]{1,0:T(8,128)S(1)} %fusion.11, bf16[320,2560]{1,0:T(8,128)(2,1)} %all_to_all.21), kind=kOutput, calls=%fused_computation.7 | convolution fusion | flops 1258618880 | bytes 2457600 | tf_op jit(solution)/shard_map/dot_general | solution.py:59
  (1 shorter events, 0.0 us)
Async XLA Ops:
  0.0 1.2 copy-start
  4.3 133.9 %all-to-all-start = ((bf16[32,10,2560]{2,1,0:T(8,128)(2,1)}), bf16[32,10,2560]{2,1,0:T(8,128)(2,1)}, u32[]{:S(2)}, u32[]{:S(2)}) async-start(bf16[32,10,2560]{2,1,0:T(8,128)(2,1)} %all_to_all.16), calls=%async_computation | async-start | bytes 5242880 | tf_op jit(solution)/shard_map/all_to_all | solution.py:46
  20.0 123.6 %collective-permute-start = (bf16[2560,384]{1,0:T(8,128)(2,1)}, bf16[2560,384]{1,0:T(8,128)(2,1)}, u32[]{:S(2)}, u32[]{:S(2)}) collective-permute-start(bf16[2560,384]{1,0:T(8,128)(2,1)} %param.9), channel_id=1, source_target_pairs={{0,1},{1,0},{2,3},{3,2},{4,5},{5,4},{6,7},{7,6},{8,9},{9,8},{10,11... | collective-permute-start | bytes 5898248 | tf_op jit(solution)/shard_map/ppermute | solution.py:11
  23.6 128.2 %collective-permute-start.1 = (bf16[2560,384]{1,0:T(8,128)(2,1)}, bf16[2560,384]{1,0:T(8,128)(2,1)}, u32[]{:S(2)}, u32[]{:S(2)}) collective-permute-start(bf16[2560,384]{1,0:T(8,128)(2,1)} %param.10), channel_id=1, source_target_pairs={{0,1},{1,0},{2,3},{3,2},{4,5},{5,4},{6,7},{7,6},{8,9},{9,8},{10,11... | collective-permute-start | bytes 5898248 | tf_op jit(solution)/shard_map/ppermute | solution.py:11
  25.8 150.6 %collective-permute-start.2 = (bf16[384,2560]{1,0:T(8,128)(2,1)}, bf16[384,2560]{1,0:T(8,128)(2,1)}, u32[]{:S(2)}, u32[]{:S(2)}) collective-permute-start(bf16[384,2560]{1,0:T(8,128)(2,1)} %param.11), channel_id=1, source_target_pairs={{0,1},{1,0},{2,3},{3,2},{4,5},{5,4},{6,7},{7,6},{8,9},{9,8},{10,11... | collective-permute-start | bytes 5898248 | tf_op jit(solution)/shard_map/ppermute | solution.py:11
  186.7 12.1 %copy-start.1 = (f32[128,2]{0,1:T(2,128)S(1)}, f32[128,2]{0,1:T(2,128)}, u32[]{:S(2)}) copy-start(f32[128,2]{0,1:T(2,128)} %param.8) | copy-start | bytes 3076
  186.7 129.6 %all-to-all-start.1 = ((bf16[32,10,2560]{2,1,0:T(8,128)(2,1)}), bf16[32,10,2560]{2,1,0:T(8,128)(2,1)S(1)}, u32[]{:S(2)}, u32[]{:S(2)}) async-start(bf16[32,10,2560]{2,1,0:T(8,128)(2,1)} %all_to_all.19), calls=%async_computation.1 | async-start | bytes 5242880 | tf_op jit(solution)/shard_map/all_to_all | solution.py:51
where the time goes:
time: 322 us
  waiting for transfers between devices  250 us (78%)
  starting transfers between devices  37.2 us (12%)
  matrix products  21.9 us (7%)
  local copies, waits for them, and re-layouts  12.1 us (4%)
    all_to_all x1, waiting for transfers between devices, per_device(): lax.all_to_all(expert_out, 'expert', split_axis=0, concat_axis=0, tiled=T...  117 us
    all_to_all x1, waiting for transfers between devices, per_device(): lax.all_to_all(slot_rows, 'expert', split_axis=0, concat_axis=0, tiled=True)  109 us
    ppermute x3, waiting for transfers between devices, partner(): lax.ppermute(value, axis, [(i, i ^ 1 << stride) for i in range(lax.axis_s...  24.6 us
    all_to_all x1, starting transfers between devices, per_device(): lax.all_to_all(slot_rows, 'expert', split_axis=0, concat_axis=0, tiled=True)  15.7 us
    all_to_all x1, starting transfers between devices, per_device(): lax.all_to_all(expert_out, 'expert', split_axis=0, concat_axis=0, tiled=T...  12.1 us
    dot_general x2, matrix products, expert_part(): jnp.dot(hidden, down_rows, preferred_element_type=jnp.float32)  12 us
    ppermute x3, starting transfers between devices, partner(): lax.ppermute(value, axis, [(i, i ^ 1 << stride) for i in range(lax.axis_s...  9.48 us
  transfers between devices with their start and end apart: 5, of which 3 were waited for; matrix products, arithmetic and copies ran while one was open for 4% of the time, Pallas kernels for 0%

commit v1 on v0

v1 whole, which is shorter than its diff:
```python
import jax
import jax.numpy as jnp
from jax import lax
from jax.experimental import pallas as pl
from jax.experimental.pallas import tpu as pltpu
from jax.sharding import PartitionSpec as P


D = 2560
HID = 384
TOK = 128
CAP = 20
BLK = 2 * CAP
NB = 8
ROWS = NB * BLK
AXES = ("dp", "expert")
VMEM = pl.BlockSpec(memory_space=pltpu.VMEM)
SMEM = pl.BlockSpec(memory_space=pltpu.SMEM)
BLOCKS = (
    ((0, 4), (0, 3), (1, 3), (0, 2), (1, 2), (0, 1), (1, 1), (0, 0)),
    ((1, -4), (1, -3), (0, -3), (1, -2), (0, -2), (1, -1), (0, -1), (1, 0)),
)


def pairs_of(move):
    def index(x, y, z, c):
        return ((x % 4) * 8 + (z % 32) // 8 * 2 + c) * 32 + (z % 8) * 4 + y % 4

    return sorted(
        (index(x, y, z, c), index(*move(x, y, z, c)))
        for x in range(4)
        for y in range(4)
        for z in range(32)
        for c in range(2)
    )


def block_move(k):
    def move(x, y, z, c):
        far, away = BLOCKS[c][k]
        return x, 3 - y if far else y, z + away, c

    return move


def send(value, move, back=False):
    pairs = pairs_of(move)
    if back:
        pairs = sorted((b, a) for a, b in pairs)
    return lax.ppermute(value, AXES, pairs)


def other_core(x, y, z, c):
    return x, y, z, 1 - c


def pair_y(x, y, z, c):
    return x, y ^ 1, z, c


def pair_x(x, y, z, c):
    return x ^ 1, y, z, c


def places(small, experts):
    hit0 = small[0:1, :] == experts
    hit1 = small[1:2, :] == experts
    hit = hit0 | hit1
    src = lax.broadcasted_iota(jnp.int32, (TOK, TOK), 0)
    dst = lax.broadcasted_iota(jnp.int32, (TOK, TOK), 1)
    before = (src < dst).astype(jnp.bfloat16)
    rank = jnp.dot(
        hit.astype(jnp.float32).astype(jnp.bfloat16),
        before,
        preferred_element_type=jnp.float32,
    )
    weight = jnp.where(hit0, small[2:3, :], small[3:4, :])
    return jnp.where(hit, rank, -1.0), weight


def chooser(own, other, experts, weighted):
    own_pos, own_w = places(own[...], experts[...])
    other_pos, other_w = places(other[...], experts[...])
    pos = jnp.concatenate([own_pos, other_pos], axis=1)
    weight = jnp.concatenate([own_w, other_w], axis=1)
    row = lax.broadcasted_iota(jnp.int32, (BLK, 2 * TOK), 0)
    lane = lax.broadcasted_iota(jnp.int32, (BLK, 2 * TOK), 1)
    slot = jnp.where(
        lane < TOK,
        jnp.where(row < CAP, row, -2),
        jnp.where(row >= CAP, row - CAP, -2),
    ).astype(jnp.float32)
    parts = []
    for b in range(NB):
        value = weight[b : b + 1, :] if weighted else 1.0
        parts.append(jnp.where(pos[b : b + 1, :] == slot, value, 0.0))
    return jnp.concatenate(parts, axis=0)


def gather_kernel(own_small, other_small, experts, own_tok, other_tok, *outs):
    choose = chooser(own_small, other_small, experts, False).astype(jnp.bfloat16)
    step = 512
    for lo in range(0, D, step):
        cols = slice(lo, lo + step)
        rows = jnp.dot(
            choose[:, :TOK], own_tok[:, cols], preferred_element_type=jnp.float32
        ) + jnp.dot(
            choose[:, TOK:], other_tok[:, cols], preferred_element_type=jnp.float32
        )
        for b in range(NB):
            outs[b][:, cols] = rows[b * BLK : (b + 1) * BLK].astype(jnp.bfloat16)


def gather(own_small, other_small, experts, own_tok, other_tok):
    return pl.pallas_call(
        gather_kernel,
        out_shape=[jax.ShapeDtypeStruct((BLK, D), jnp.bfloat16)] * NB,
        in_specs=[VMEM] * 5,
        out_specs=[VMEM] * NB,
        name="gather_rows",
    )(own_small, other_small, experts, own_tok, other_tok)


def mixer_kernel(own_small, other_small, experts, high, low):
    mix = chooser(own_small, other_small, experts, True).T
    rounded = mix.astype(jnp.bfloat16)
    high[...] = rounded
    low[...] = (mix - rounded.astype(jnp.float32)).astype(jnp.bfloat16)


def mixer(own_small, other_small, experts):
    return pl.pallas_call(
        mixer_kernel,
        out_shape=[jax.ShapeDtypeStruct((2 * TOK, ROWS), jnp.bfloat16)] * 2,
        in_specs=[VMEM] * 3,
        out_specs=[VMEM] * 2,
        name="mix_matrix",
    )(own_small, other_small, experts)


def join(blocks, rows):
    for b in range(NB):
        rows[b * BLK : (b + 1) * BLK, :] = blocks[b][...]


def act(gate, up):
    return (gate / (1.0 + jnp.exp(-gate)) * up).astype(jnp.bfloat16)


def hidden_own_kernel(w_gate, w_up, *refs):
    blocks, hidden, rows = refs[:NB], refs[NB], refs[NB + 1]
    join(blocks, rows)
    x = rows[...]
    gate = jnp.dot(x, w_gate[...], preferred_element_type=jnp.float32)
    up = jnp.dot(x, w_up[...], preferred_element_type=jnp.float32)
    hidden[...] = act(gate, up)


def hidden_own(w_gate, w_up, blocks):
    return pl.pallas_call(
        hidden_own_kernel,
        out_shape=jax.ShapeDtypeStruct((ROWS, HID), jnp.bfloat16),
        in_specs=[VMEM] * (2 + NB),
        out_specs=VMEM,
        scratch_shapes=[pltpu.VMEM((ROWS, D), jnp.bfloat16)],
        name="hidden_own",
    )(w_gate, w_up, *blocks)


def hidden_other_kernel(starts, *refs):
    pieces, blocks, hidden, rows = refs[:4], refs[4 : 4 + NB], refs[4 + NB], refs[5 + NB]
    join(blocks, rows)
    gate = jnp.zeros((ROWS, HID), jnp.float32)
    up = jnp.zeros((ROWS, HID), jnp.float32)
    for k, piece in enumerate(pieces):
        x = rows[:, pl.ds(pl.multiple_of(starts[k], 128), D // 4)]
        gate = gate + jnp.dot(x, piece[0], preferred_element_type=jnp.float32)
        up = up + jnp.dot(x, piece[1], preferred_element_type=jnp.float32)
    hidden[...] = act(gate, up)


def hidden_other(starts, pieces, blocks):
    return pl.pallas_call(
        hidden_other_kernel,
        out_shape=jax.ShapeDtypeStruct((ROWS, HID), jnp.bfloat16),
        in_specs=[SMEM] + [VMEM] * (4 + NB),
        out_specs=VMEM,
        scratch_shapes=[pltpu.VMEM((ROWS, D), jnp.bfloat16)],
        name="hidden_other",
    )(starts, *pieces, *blocks)


def down_kernel(starts, own_hidden, other_hidden, w_down, *refs):
    pieces, outs = refs[:4], refs[4:]
    for k, piece in enumerate(pieces):
        cols = pl.ds(pl.multiple_of(starts[k], 128), D // 4)
        result = jnp.dot(
            own_hidden[...], w_down[:, cols], preferred_element_type=jnp.float32
        ) + jnp.dot(other_hidden[...], piece[...], preferred_element_type=jnp.float32)
        for b in range(NB):
            outs[b][:, cols] = result[b * BLK : (b + 1) * BLK].astype(jnp.bfloat16)


def down(starts, own_hidden, other_hidden, w_down, pieces):
    return pl.pallas_call(
        down_kernel,
        out_shape=[jax.ShapeDtypeStruct((BLK, D), jnp.bfloat16)] * NB,
        in_specs=[SMEM] + [VMEM] * 7,
        out_specs=[VMEM] * NB,
        name="down_rows",
    )(starts, own_hidden, other_hidden, w_down, *pieces)


def mixed(high, low, part):
    return jnp.dot(high, part, preferred_element_type=jnp.float32) + jnp.dot(
        low, part, preferred_element_type=jnp.float32
    )


def mix_other_kernel(high, low, *refs):
    blocks, other, rows = refs[:NB], refs[NB], refs[NB + 1]
    join(blocks, rows)
    step = 512
    for lo in range(0, D, step):
        cols = slice(lo, lo + step)
        other[:, cols] = mixed(high[TOK:], low[TOK:], rows[:, cols]).astype(
            jnp.bfloat16
        )


def mix_own_kernel(high, low, *refs):
    blocks, own, rows = refs[:NB], refs[NB], refs[NB + 1]
    join(blocks, rows)
    step = 512
    for lo in range(0, D, step):
        cols = slice(lo, lo + step)
        own[:, cols] = mixed(high[:TOK], low[:TOK], rows[:, cols])


def mix(kernel, dtype, high, low, blocks):
    return pl.pallas_call(
        kernel,
        out_shape=jax.ShapeDtypeStruct((TOK, D), dtype),
        in_specs=[VMEM] * (2 + NB),
        out_specs=VMEM,
        scratch_shapes=[pltpu.VMEM((ROWS, D), jnp.bfloat16)],
    )(high, low, *blocks)


def layer(tokens, expert_ids, gate_weights, w_gate, w_up, w_down):
    place, part = lax.axis_index("expert"), lax.axis_index("dp")
    core, x_odd = part % 2, (part // 8) % 2
    z, y = place // 4, place % 4
    far = jnp.where(core == 0, *(jnp.array([f for f, _ in BLOCKS[c]]) for c in range(2)))
    away = jnp.where(core == 0, *(jnp.array([a for _, a in BLOCKS[c]]) for c in range(2)))
    expert = ((z + away + 8) % 8) * 2 + (far ^ (y // 2))
    experts = jnp.broadcast_to(expert.astype(jnp.float32)[:, None], (NB, TOK))
    small = jnp.concatenate(
        [
            expert_ids.T.astype(jnp.float32),
            gate_weights.T,
            jnp.zeros((4, TOK), jnp.float32),
        ]
    )
    other_tok = send(tokens, other_core)
    other_small = send(small, other_core)
    blocks = gather(small, other_small, experts, tokens, other_tok)

    piece = x_odd * 2 + core
    rows_at = piece * (D // 4)
    gate_up = jnp.stack(
        [
            lax.dynamic_slice(w_gate, (rows_at, 0), (D // 4, HID)),
            lax.dynamic_slice(w_up, (rows_at, 0), (D // 4, HID)),
        ]
    )
    down_cols = lax.dynamic_slice(w_down, (0, rows_at), (HID, D // 4))
    gu0 = send(gate_up, pair_y)
    dn0 = send(down_cols, pair_y)
    gu1 = send(gu0, pair_x)
    dn1 = send(dn0, pair_x)
    gu2 = send(gu0, other_core)
    gu3 = send(gu1, other_core)
    dn2 = send(dn0, other_core)
    dn3 = send(dn1, other_core)
    starts = jnp.stack(
        [
            (a * 2 + b) * (D // 4)
            for a, b in (
                (x_odd, core),
                (1 - x_odd, core),
                (x_odd, 1 - core),
                (1 - x_odd, 1 - core),
            )
        ]
    ).astype(jnp.int32)

    arrived = []
    for k in range(NB):
        arrived.append(send(blocks[k], block_move(k)))
    high, low = mixer(small, other_small, experts)
    h_own = hidden_own(w_gate, w_up, arrived)
    h_other = hidden_other(starts, (gu0, gu1, gu2, gu3), arrived)
    results = down(starts, h_own, h_other, w_down, (dn0, dn1, dn2, dn3))
    returned = []
    for k in range(NB):
        returned.append(send(results[k], block_move(k), back=True))
    theirs = mix(mix_other_kernel, jnp.bfloat16, high, low, returned)
    rest = send(theirs, other_core)
    mine = mix(mix_own_kernel, jnp.float32, high, low, returned)
    return (mine + rest.astype(jnp.float32)).astype(jnp.bfloat16)


def solution(mesh):
    in_specs = (
        P(AXES, None),
        P(AXES, None),
        P(AXES, None),
        P(None, "expert"),
        P(None, "expert"),
        P("expert", None),
    )
    return jax.shard_map(
        layer,
        mesh=mesh,
        in_specs=in_specs,
        out_specs=P(AXES, None),
        check_vma=False,
    )
```

time: 322 us -> 205 us (0.64)
  the two profiles are of different devices: /device:TPU:258 before, /device:TPU:1 now
where the time goes in v1:
time: 205 us; the launch traced here: 204 us
  starting transfers between devices  127 us (62%)
  waiting for transfers between devices  39.4 us (19%)
  Pallas kernels  28.1 us (14%)
  local copies, waits for them, and re-layouts  5.78 us (3%)
  other arithmetic  3.08 us (2%)
    ppermute x27, starting transfers between devices, send(): return lax.ppermute(value, AXES, pairs)  127 us
    ppermute x27, waiting for transfers between devices, send(): return lax.ppermute(value, AXES, pairs)  39.4 us
    pallas_call x2, Pallas kernels, mix(): pl.pallas_call(kernel, out_shape=jax.ShapeDtypeStruct((TOK, D), dtype), i...  6.85 us
    pallas_call x1, Pallas kernels, down(): pl.pallas_call(down_kernel, out_shape=[jax.ShapeDtypeStruct((BLK, D), jnp...  5.49 us
    pallas_call x1, Pallas kernels, hidden_other(): pl.pallas_call(hidden_other_kernel, out_shape=jax.ShapeDtypeStruct((ROWS,...  5.39 us
    pallas_call x1, Pallas kernels, hidden_own(): pl.pallas_call(hidden_own_kernel, out_shape=jax.ShapeDtypeStruct((ROWS, H...  5.1 us
  transfers between devices with their start and end apart: 27, of which 13 were waited for; matrix products, arithmetic and copies ran while one was open for 2% of the time, Pallas kernels for 9%

profile of v1, /device:TPU:1, one launch (start us, length us, event | category | flops | bytes accessed | tf_op | source)
XLA Modules:
  0.0 204.0 jit_solution(9896829987801380310)
XLA Ops:
  0.0 1.3 dynamic-slice_bitcast_fusion
  1.3 0.0 copy-start.17
  1.4 0.0 copy-start.18
  1.4 0.0 copy-start.19
  1.4 0.0 copy-start.20
  1.4 0.0 copy-start.21
  1.4 0.0 copy-start.22
  1.4 0.1 pad_maximum_fusion
  1.5 4.0 %collective-permute-start.10 = (bf16[2,640,384]{2,1,0:T(8,128)(2,1)S(1)}, bf16[2,640,384]{2,1,0:T(8,128)(2,1)S(1)}, u32[]{:S(2)}, u32[]{:S(2)}) collective-permute-start(bf16[2,640,384]{2,1,0:T(8,128)(2,1)S(1)} %pad_maximum_fusion), channel_id=1, source_target_pairs={{0,1},{1,0},{2,3},{3,2},{4,5},{5,4},{6,7},{7,6},{8,9},{9,8},{10,11... | collective-permute-start | bytes 2949128 | tf_op jit(solution)/shard_map/ppermute | solution.py:50
  5.6 11.5 %collective-permute-done.10.refs_0_ = bf16[2,640,384]{2,1,0:T(8,128)(2,1)S(1)} collective-permute-done((bf16[2,640,384]{2,1,0:T(8,128)(2,1)S(1)}, bf16[2,640,384]{2,1,0:T(8,128)(2,1)S(1)}, u32[]{:S(2)}, u32[]{:S(2)}) %collective-permute-start.10) | collective-permute-done | bytes 983072 | tf_op jit(solution)/shard_map/ppermute | solution.py:50
  17.0 13.0 %collective-permute-start.11 = (bf16[2,640,384]{2,1,0:T(8,128)(2,1)S(1)}, bf16[2,640,384]{2,1,0:T(8,128)(2,1)S(1)}, u32[]{:S(2)}, u32[]{:S(2)}) collective-permute-start(bf16[2,640,384]{2,1,0:T(8,128)(2,1)S(1)} %collective-permute-done.10.refs_0_), channel_id=1, source_target_pairs={{0,256},{1,257},{2,258},{3,259},{4,260},{5,261},{6,262},{7,263},{8... | collective-permute-start | bytes 2949128 | tf_op jit(solution)/shard_map/ppermute | solution.py:50
  30.0 5.5 %collective-permute-start.1 = (bf16[128,2560]{1,0:T(8,128)(2,1)S(1)}, bf16[128,2560]{1,0:T(8,128)(2,1)S(1)}, u32[]{:S(2)}, u32[]{:S(2)}) collective-permute-start(bf16[128,2560]{1,0:T(8,128)(2,1)S(1)} %copy-done.13), channel_id=1, source_target_pairs={{0,32},{1,33},{2,34},{3,35},{4,36},{5,37},{6,38},{7,39},{8,40},{9,... | collective-permute-start | bytes 1966088 | tf_op jit(solution)/shard_map/ppermute | solution.py:50
  35.5 1.9 constant_dynamic-slice_fusion
  37.3 1.9 collective-permute-start.14
  39.3 0.1 pad.8.clone
  39.4 0.1 maximum_maximum_fusion.own_small
  39.4 1.9 collective-permute-start
  41.5 1.0 collective-permute-done.other_small
  42.5 0.7 broadcast_in_dim.10.experts
  43.2 0.1 copy-done.14
  43.3 3.5 %gather_rows.1 = (bf16[40,2560]{1,0:T(8,128)(2,1)}, bf16[40,2560]{1,0:T(8,128)(2,1)}, bf16[40,2560]{1,0:T(8,128)(2,1)}, bf16[40,2560]{1,0:T(8,128)(2,1)}, bf16[4...) custom-call(f32[8,128]{1,0:T(8,128)} %copy-done.15, ...), custom_call_target="tpu_custom_call" | custom-call | tf_op jit(solution)/shard_map/gather_rows/pallas_call | solution.py:115
  46.8 20.9 %collective-permute-start.2 = (bf16[40,2560]{1,0:T(8,128)(2,1)}, bf16[40,2560]{1,0:T(8,128)(2,1)S(1)}, u32[]{:S(2)}, u32[]{:S(2)}) collective-permute-start(bf16[40,2560]{1,0:T(8,128)(2,1)} %get-tuple-element.25), channel_id=1, source_target_pairs={{0,16},{1,17},{2,18},{3,19},{4,20},{5,21},{6,22},{7,23},{8,24},{9,... | collective-permute-start | bytes 614408 | tf_op jit(solution)/shard_map/ppermute | solution.py:50
  67.7 5.2 %collective-permute-start.3 = (bf16[40,2560]{1,0:T(8,128)(2,1)}, bf16[40,2560]{1,0:T(8,128)(2,1)S(1)}, u32[]{:S(2)}, u32[]{:S(2)}) collective-permute-start(bf16[40,2560]{1,0:T(8,128)(2,1)} %get-tuple-element.26), channel_id=1, source_target_pairs={{0,12},{1,13},{2,14},{3,15},{4,16},{5,17},{6,18},{7,19},{8,20},{9,... | collective-permute-start | bytes 614408 | tf_op jit(solution)/shard_map/ppermute | solution.py:50
  73.0 1.9 collective-permute-start.12
  74.9 2.4 %collective-permute-start.13 = (bf16[2,640,384]{2,1,0:T(8,128)(2,1)S(1)}, bf16[2,640,384]{2,1,0:T(8,128)(2,1)}, u32[]{:S(2)}, u32[]{:S(2)}) collective-permute-start(bf16[2,640,384]{2,1,0:T(8,128)(2,1)S(1)} %collective-permute-done.11.refs_1_), channel_id=1, source_target_pairs={{0,32},{1,33},{2,34},{3,35},{4,36},{5,37},{6,38},{7,39},{8,40},{9,... | collective-permute-start | bytes 2949128 | tf_op jit(solution)/shard_map/ppermute | solution.py:50
  77.3 2.2 %collective-permute-start.15 = (bf16[384,640]{1,0:T(8,128)(2,1)}, bf16[384,640]{1,0:T(8,128)(2,1)}, u32[]{:S(2)}, u32[]{:S(2)}) collective-permute-start(bf16[384,640]{1,0:T(8,128)(2,1)} %collective-permute-done.14.refs_0_), channel_id=1, source_target_pairs={{0,256},{1,257},{2,258},{3,259},{4,260},{5,261},{6,262},{7,263},{8... | collective-permute-start | bytes 1474568 | tf_op jit(solution)/shard_map/ppermute | solution.py:50
  79.5 5.3 %collective-permute-start.4 = (bf16[40,2560]{1,0:T(8,128)(2,1)}, bf16[40,2560]{1,0:T(8,128)(2,1)}, u32[]{:S(2)}, u32[]{:S(2)}) collective-permute-start(bf16[40,2560]{1,0:T(8,128)(2,1)} %get-tuple-element.27), channel_id=1, source_target_pairs={{0,15},{1,14},{2,13},{3,12},{4,19},{5,18},{6,17},{7,16},{8,23},{9,... | collective-permute-start | bytes 614408 | tf_op jit(solution)/shard_map/ppermute | solution.py:50
  84.9 5.3 %collective-permute-start.5 = (bf16[40,2560]{1,0:T(8,128)(2,1)}, bf16[40,2560]{1,0:T(8,128)(2,1)}, u32[]{:S(2)}, u32[]{:S(2)}) collective-permute-start(bf16[40,2560]{1,0:T(8,128)(2,1)} %get-tuple-element.28), channel_id=1, source_target_pairs={{0,8},{1,9},{2,10},{3,11},{4,12},{5,13},{6,14},{7,15},{8,16},{9,17... | collective-permute-start | bytes 614408 | tf_op jit(solution)/shard_map/ppermute | solution.py:50
  90.1 3.8 %collective-permute-done.4.refs_2_.refs_6_ = bf16[40,2560]{1,0:T(8,128)(2,1)} collective-permute-done((bf16[40,2560]{1,0:T(8,128)(2,1)}, bf16[40,2560]{1,0:T(8,128)(2,1)}, u32[]{:S(2)}, u32[]{:S(2)}) %collective-permute-start.4) | collective-permute-done | bytes 204832 | tf_op jit(solution)/shard_map/ppermute | solution.py:50
  93.9 3.7 %collective-permute-start.6 = (bf16[40,2560]{1,0:T(8,128)(2,1)}, bf16[40,2560]{1,0:T(8,128)(2,1)}, u32[]{:S(2)}, u32[]{:S(2)}) collective-permute-start(bf16[40,2560]{1,0:T(8,128)(2,1)} %get-tuple-element.29), channel_id=1, source_target_pairs={{0,11},{1,10},{2,9},{3,8},{4,15},{5,14},{6,13},{7,12},{8,19},{9,18... | collective-permute-start | bytes 614408 | tf_op jit(solution)/shard_map/ppermute | solution.py:50
  97.7 0.5 collective-permute-done.5.refs_3_.refs_7_
  98.2 8.1 %collective-permute-start.7 = (bf16[40,2560]{1,0:T(8,128)(2,1)}, bf16[40,2560]{1,0:T(8,128)(2,1)}, u32[]{:S(2)}, u32[]{:S(2)}) collective-permute-start(bf16[40,2560]{1,0:T(8,128)(2,1)} %get-tuple-element.30), channel_id=1, source_target_pairs={{0,4},{1,5},{2,6},{3,7},{4,8},{5,9},{6,10},{7,11},{8,12},{9,13},{1... | collective-permute-start | bytes 614408 | tf_op jit(solution)/shard_map/ppermute | solution.py:50
  106.3 7.1 %collective-permute-start.16 = (bf16[384,640]{1,0:T(8,128)(2,1)}, bf16[384,640]{1,0:T(8,128)(2,1)}, u32[]{:S(2)}, u32[]{:S(2)}) collective-permute-start(bf16[384,640]{1,0:T(8,128)(2,1)} %collective-permute-done.14.refs_0_), channel_id=1, source_target_pairs={{0,32},{1,33},{2,34},{3,35},{4,36},{5,37},{6,38},{7,39},{8,40},{9,... | collective-permute-start | bytes 1474568 | tf_op jit(solution)/shard_map/ppermute | solution.py:50
  113.4 1.9 collective-permute-start.17
  115.3 1.9 collective-permute-start.8
  117.3 6.1 %collective-permute-done.8.refs_6_.refs_10_ = bf16[40,2560]{1,0:T(8,128)(2,1)} collective-permute-done((bf16[40,2560]{1,0:T(8,128)(2,1)}, bf16[40,2560]{1,0:T(8,128)(2,1)}, u32[]{:S(2)}, u32[]{:S(2)}) %collective-permute-start.8) | collective-permute-done | bytes 204832 | tf_op jit(solution)/shard_map/ppermute | solution.py:50
  123.3 2.8 %collective-permute-start.9 = (bf16[40,2560]{1,0:T(8,128)(2,1)}, bf16[40,2560]{1,0:T(8,128)(2,1)}, u32[]{:S(2)}, u32[]{:S(2)}) collective-permute-start(bf16[40,2560]{1,0:T(8,128)(2,1)} %get-tuple-element.32), channel_id=1, source_target_pairs={{0,0},{1,1},{2,2},{3,3},{4,4},{5,5},{6,6},{7,7},{8,8},{9,9},{10,10... | collective-permute-start | bytes 614408 | tf_op jit(solution)/shard_map/ppermute | solution.py:50
  126.1 0.6 pad_add_fusion.starts
  126.7 4.6 %collective-permute-done.9.refs_7_.refs_11_ = bf16[40,2560]{1,0:T(8,128)(2,1)} collective-permute-done((bf16[40,2560]{1,0:T(8,128)(2,1)}, bf16[40,2560]{1,0:T(8,128)(2,1)}, u32[]{:S(2)}, u32[]{:S(2)}) %collective-permute-start.9) | collective-permute-done | bytes 204832 | tf_op jit(solution)/shard_map/ppermute | solution.py:50
  131.4 5.1 %hidden_own.1.own_hidden = bf16[320,384]{1,0:T(8,128)(2,1)} custom-call(bf16[2560,384]{1,0:T(8,128)(2,1)} %w_gate.1, bf16[2560,384]{1,0:T(8,128)(2,1)} %w_up.1, bf16[40,2560]{1,0:T(8,128)(2,1)} %copy-done.11, bf16[40,2560]{1,0:T(8,128)(2,1)} %copy-done.12, bf16[40,2560]{1,0:T(8,128)(2,1)} %collective-permute-done.4.refs_2_.refs_6_, ...), custom_call_target="tpu_custom_call" | custom-call | tf_op jit(solution)/shard_map/hidden_own/pallas_call | solution.py:160
  136.5 0.9 copy-done.2
  137.4 5.4 %hidden_other.1.other_hidden = bf16[320,384]{1,0:T(8,128)(2,1)} custom-call(s32[4]{0:T(128)} %pad_add_fusion.starts, bf16[2,640,384]{2,1,0:T(8,128)(2,1)} %copy-done, bf16[2,640,384]{2,1,0:T(8,128)(2,1)} %copy-done.1, bf16[2,640,384]{2,1,0:T(8,128)(2,1)} %copy-done.2, bf16[2,640,384]{2,1,0:T(8,128)(2,1)} %collective-permute-done.13.refs_3_, ...), custom_call_target="tpu_custom_call" | custom-call | tf_op jit(solution)/shard_map/hidden_other/pallas_call | solution.py:183
  142.8 5.5 %down_rows.1 = (bf16[40,2560]{1,0:T(8,128)(2,1)}, bf16[40,2560]{1,0:T(8,128)(2,1)}, bf16[40,2560]{1,0:T(8,128)(2,1)}, bf16[40,2560]{1,0:T(8,128)(2,1)}, bf16[40,...) custom-call(s32[4]{0:T(128)} %pad_add_fusion.starts, ...), custom_call_target="tpu_custom_call" | custom-call | tf_op jit(solution)/shard_map/down_rows/pallas_call | solution.py:205
  148.3 4.7 %collective-permute-start.18 = (bf16[40,2560]{1,0:T(8,128)(2,1)}, bf16[40,2560]{1,0:T(8,128)(2,1)S(1)}, u32[]{:S(2)}, u32[]{:S(2)}) collective-permute-start(bf16[40,2560]{1,0:T(8,128)(2,1)} %get-tuple-element.33), channel_id=1, source_target_pairs={{0,208},{1,209},{2,210},{3,211},{4,212},{5,213},{6,214},{7,215},{8... | collective-permute-start | bytes 614408 | tf_op jit(solution)/shard_map/ppermute | solution.py:50
  153.0 4.9 %collective-permute-start.19 = (bf16[40,2560]{1,0:T(8,128)(2,1)}, bf16[40,2560]{1,0:T(8,128)(2,1)S(1)}, u32[]{:S(2)}, u32[]{:S(2)}) collective-permute-start(bf16[40,2560]{1,0:T(8,128)(2,1)} %get-tuple-element.34), channel_id=1, source_target_pairs={{0,212},{1,213},{2,214},{3,215},{4,216},{5,217},{6,218},{7,219},{8... | collective-permute-start | bytes 614408 | tf_op jit(solution)/shard_map/ppermute | solution.py:50
  157.9 3.4 %collective-permute-start.20 = (bf16[40,2560]{1,0:T(8,128)(2,1)}, bf16[40,2560]{1,0:T(8,128)(2,1)S(1)}, u32[]{:S(2)}, u32[]{:S(2)}) collective-permute-start(bf16[40,2560]{1,0:T(8,128)(2,1)} %get-tuple-element.35), channel_id=1, source_target_pairs={{0,215},{1,214},{2,213},{3,212},{4,219},{5,218},{6,217},{7,216},{8... | collective-permute-start | bytes 614408 | tf_op jit(solution)/shard_map/ppermute | solution.py:50
  161.3 4.9 %collective-permute-start.21 = (bf16[40,2560]{1,0:T(8,128)(2,1)}, bf16[40,2560]{1,0:T(8,128)(2,1)S(1)}, u32[]{:S(2)}, u32[]{:S(2)}) collective-permute-start(bf16[40,2560]{1,0:T(8,128)(2,1)} %get-tuple-element.36), channel_id=1, source_target_pairs={{0,216},{1,217},{2,218},{3,219},{4,220},{5,221},{6,222},{7,223},{8... | collective-permute-start | bytes 614408 | tf_op jit(solution)/shard_map/ppermute | solution.py:50
  166.2 2.3 %collective-permute-start.22 = (bf16[40,2560]{1,0:T(8,128)(2,1)}, bf16[40,2560]{1,0:T(8,128)(2,1)S(1)}, u32[]{:S(2)}, u32[]{:S(2)}) collective-permute-start(bf16[40,2560]{1,0:T(8,128)(2,1)} %get-tuple-element.37), channel_id=1, source_target_pairs={{0,219},{1,218},{2,217},{3,216},{4,223},{5,222},{6,221},{7,220},{8... | collective-permute-start | bytes 614408 | tf_op jit(solution)/shard_map/ppermute | solution.py:50
  168.6 0.7 collective-permute-done.18.refs_0_
  169.2 4.6 %collective-permute-start.23 = (bf16[40,2560]{1,0:T(8,128)(2,1)}, bf16[40,2560]{1,0:T(8,128)(2,1)S(1)}, u32[]{:S(2)}, u32[]{:S(2)}) collective-permute-start(bf16[40,2560]{1,0:T(8,128)(2,1)} %get-tuple-element.38), channel_id=1, source_target_pairs={{0,220},{1,221},{2,222},{3,223},{4,0},{5,1},{6,2},{7,3},{8,4},{9,5... | collective-permute-start | bytes 614408 | tf_op jit(solution)/shard_map/ppermute | solution.py:50
  173.8 0.7 collective-permute-done.19.refs_1_
  174.5 3.6 %collective-permute-start.24 = (bf16[40,2560]{1,0:T(8,128)(2,1)}, bf16[40,2560]{1,0:T(8,128)(2,1)S(1)}, u32[]{:S(2)}, u32[]{:S(2)}) collective-permute-start(bf16[40,2560]{1,0:T(8,128)(2,1)} %get-tuple-element.39), channel_id=1, source_target_pairs={{0,223},{1,222},{2,221},{3,220},{4,3},{5,2},{6,1},{7,0},{8,7},{9,6... | collective-permute-start | bytes 614408 | tf_op jit(solution)/shard_map/ppermute | solution.py:50
  178.2 1.8 collective-permute-done.20.refs_2_
  180.0 1.9 collective-permute-start.25
  181.9 1.8 mix_matrix.1
  183.7 0.4 collective-permute-done.21.refs_3_
  184.1 1.7 collective-permute-done.22.refs_4_
  185.8 5.8 %collective-permute-done.23.refs_5_ = bf16[40,2560]{1,0:T(8,128)(2,1)S(1)} collective-permute-done((bf16[40,2560]{1,0:T(8,128)(2,1)}, bf16[40,2560]{1,0:T(8,128)(2,1)S(1)}, u32[]{:S(2)}, u32[]{:S(2)}) %collective-permute-start.23) | collective-permute-done | bytes 204832 | tf_op jit(solution)/shard_map/ppermute | solution.py:50
  191.6 0.7 collective-permute-done.25.refs_7_
  192.4 0.6 copy-done.10
  193.0 3.3 %shard_map.101 = bf16[128,2560]{1,0:T(8,128)(2,1)} custom-call(bf16[256,320]{1,0:T(8,128)(2,1)} %get-tuple-element.23.high, bf16[256,320]{1,0:T(8,128)(2,1)} %get-tuple-element.24.low, bf16[40,2560]{1,0:T(8,128)(2,1)} %copy-done.3, bf16[40,2560]{1,0:T(8,128)(2,1)} %copy-done.4, bf16[40,2560]{1,0:T(8,128)(2,1)} %copy-done.5, bf16[40,2560]{1,0:T(8,128)(2,1)} %copy-done.6, ...), custom_call_target="tpu_custom_call" | custom-call | tf_op jit(solution)/shard_map/pallas_call | solution.py:241
  196.3 1.9 collective-permute-start.26
  198.2 3.6 %shard_map.100 = f32[128,2560]{1,0:T(8,128)} custom-call(bf16[256,320]{1,0:T(8,128)(2,1)} %get-tuple-element.23.high, bf16[256,320]{1,0:T(8,128)(2,1)} %get-tuple-element.24.low, bf16[40,2560]{1,0:T(8,128)(2,1)} %copy-done.3, bf16[40,2560]{1,0:T(8,128)(2,1)} %copy-done.4, bf16[40,2560]{1,0:T(8,128)(2,1)} %copy-done.5, bf16[40,2560]{1,0:T(8,128)(2,1)} %copy-done.6, ...), custom_call_target="tpu_custom_call" | custom-call | tf_op jit(solution)/shard_map/pallas_call | solution.py:241
  201.8 2.3 %add_convert_fusion = bf16[128,2560]{1,0:T(8,128)(2,1)} fusion(f32[128,2560]{1,0:T(8,128)} %shard_map.100, bf16[128,2560]{1,0:T(8,128)(2,1)S(1)} %collective-permute-done.26), kind=kLoop, calls=%fused_computation | loop fusion | flops 983040 | bytes 2621440 | tf_op jit(solution)/shard_map/convert_element_type | solution.py:311
  (54 shorter events, 0.1 us)
Async XLA Ops:
  0.0 30.0 %copy-start.13 = (bf16[128,2560]{1,0:T(8,128)(2,1)S(1)}, bf16[128,2560]{1,0:T(8,128)(2,1)}, u32[]{:S(2)}) copy-start(bf16[128,2560]{1,0:T(8,128)(2,1)} %own_tok.1) | copy-start | bytes 1966084
  1.3 38.0 %copy-start.17 = (s32[128,2]{0,1:T(2,128)S(1)}, s32[128,2]{0,1:T(2,128)}, u32[]{:S(2)}) copy-start(s32[128,2]{0,1:T(2,128)} %param.11) | copy-start | bytes 3076
  1.4 38.0 %copy-start.18 = (f32[128,2]{0,1:T(2,128)S(1)}, f32[128,2]{0,1:T(2,128)}, u32[]{:S(2)}) copy-start(f32[128,2]{0,1:T(2,128)} %param.12) | copy-start | bytes 3076
  1.4 40.0 %copy-start.19 = (s32[8]{0:T(128)S(1)}, s32[8]{0:T(128)}, u32[]{:S(2)}) copy-start(s32[8]{0:T(128)} %constant.93.clone) | copy-start | bytes 100
  1.4 40.0 %copy-start.20 = (s32[8]{0:T(128)S(1)}, s32[8]{0:T(128)}, u32[]{:S(2)}) copy-start(s32[8]{0:T(128)} %constant.94.clone) | copy-start | bytes 100
  1.4 40.0 %copy-start.21 = (s32[8]{0:T(128)S(1)}, s32[8]{0:T(128)}, u32[]{:S(2)}) copy-start(s32[8]{0:T(128)} %constant.95.clone) | copy-start | bytes 100
  1.4 40.0 %copy-start.22 = (s32[8]{0:T(128)S(1)}, s32[8]{0:T(128)}, u32[]{:S(2)}) copy-start(s32[8]{0:T(128)} %constant.96.clone) | copy-start | bytes 100
  1.5 15.5 %collective-permute-start.10 = (bf16[2,640,384]{2,1,0:T(8,128)(2,1)S(1)}, bf16[2,640,384]{2,1,0:T(8,128)(2,1)S(1)}, u32[]{:S(2)}, u32[]{:S(2)}) collective-permute-start(bf16[2,640,384]{2,1,0:T(8,128)(2,1)S(1)} %pad_maximum_fusion), channel_id=1, source_target_pairs={{0,1},{1,0},{2,3},{3,2},{4,5},{5,4},{6,7},{7,6},{8,9},{9,8},{10,11... | collective-permute-start | bytes 2949128 | tf_op jit(solution)/shard_map/ppermute | solution.py:50
  17.0 119.4 %copy-start = (bf16[2,640,384]{2,1,0:T(8,128)(2,1)}, bf16[2,640,384]{2,1,0:T(8,128)(2,1)S(1)}, u32[]{:S(2)}) copy-start(bf16[2,640,384]{2,1,0:T(8,128)(2,1)S(1)} %collective-permute-done.10.refs_0_) | copy-start | bytes 2949124
  17.0 57.8 %collective-permute-start.11 = (bf16[2,640,384]{2,1,0:T(8,128)(2,1)S(1)}, bf16[2,640,384]{2,1,0:T(8,128)(2,1)S(1)}, u32[]{:S(2)}, u32[]{:S(2)}) collective-permute-start(bf16[2,640,384]{2,1,0:T(8,128)(2,1)S(1)} %collective-permute-done.10.refs_0_), channel_id=1, source_target_pairs={{0,256},{1,257},{2,258},{3,259},{4,260},{5,261},{6,262},{7,263},{8... | collective-permute-start | bytes 2949128 | tf_op jit(solution)/shard_map/ppermute | solution.py:50
  30.0 12.5 %collective-permute-start.1 = (bf16[128,2560]{1,0:T(8,128)(2,1)S(1)}, bf16[128,2560]{1,0:T(8,128)(2,1)S(1)}, u32[]{:S(2)}, u32[]{:S(2)}) collective-permute-start(bf16[128,2560]{1,0:T(8,128)(2,1)S(1)} %copy-done.13), channel_id=1, source_target_pairs={{0,32},{1,33},{2,34},{3,35},{4,36},{5,37},{6,38},{7,39},{8,40},{9,... | collective-permute-start | bytes 1966088 | tf_op jit(solution)/shard_map/ppermute | solution.py:50
  37.3 40.0 %collective-permute-start.14 = (bf16[384,640]{1,0:T(8,128)(2,1)}, bf16[384,640]{1,0:T(8,128)(2,1)}, u32[]{:S(2)}, u32[]{:S(2)}) collective-permute-start(bf16[384,640]{1,0:T(8,128)(2,1)} %constant_dynamic-slice_fusion), channel_id=1, source_target_pairs={{0,1},{1,0},{2,3},{3,2},{4,5},{5,4},{6,7},{7,6},{8,9},{9,8},{10,11... | collective-permute-start | bytes 1474568 | tf_op jit(solution)/shard_map/ppermute | solution.py:50
  39.4 3.8 %copy-start.15 = (f32[8,128]{1,0:T(8,128)}, f32[8,128]{1,0:T(8,128)S(1)}, u32[]{:S(2)}) copy-start(f32[8,128]{1,0:T(8,128)S(1)} %maximum_maximum_fusion.own_small) | copy-start | bytes 12292
  39.4 3.0 %collective-permute-start = (f32[8,128]{1,0:T(8,128)S(1)}, f32[8,128]{1,0:T(8,128)S(1)}, u32[]{:S(2)}, u32[]{:S(2)}) collective-permute-start(f32[8,128]{1,0:T(8,128)S(1)} %maximum_maximum_fusion.own_small), channel_id=1, source_target_pairs={{0,32},{1,33},{2,34},{3,35},{4,36},{5,37},{6,38},{7,39},{8,40},{9,... | collective-permute-start | bytes 12296 | tf_op jit(solution)/shard_map/ppermute | solution.py:50
  42.5 0.8 copy-start.16
  42.5 0.8 copy-start.14
  46.8 32.7 %collective-permute-start.2 = (bf16[40,2560]{1,0:T(8,128)(2,1)}, bf16[40,2560]{1,0:T(8,128)(2,1)S(1)}, u32[]{:S(2)}, u32[]{:S(2)}) collective-permute-start(bf16[40,2560]{1,0:T(8,128)(2,1)} %get-tuple-element.25), channel_id=1, source_target_pairs={{0,16},{1,17},{2,18},{3,19},{4,20},{5,21},{6,22},{7,23},{8,24},{9,... | collective-permute-start | bytes 614408 | tf_op jit(solution)/shard_map/ppermute | solution.py:50
  67.7 17.1 %collective-permute-start.3 = (bf16[40,2560]{1,0:T(8,128)(2,1)}, bf16[40,2560]{1,0:T(8,128)(2,1)S(1)}, u32[]{:S(2)}, u32[]{:S(2)}) collective-permute-start(bf16[40,2560]{1,0:T(8,128)(2,1)} %get-tuple-element.26), channel_id=1, source_target_pairs={{0,12},{1,13},{2,14},{3,15},{4,16},{5,17},{6,18},{7,19},{8,20},{9,... | collective-permute-start | bytes 614408 | tf_op jit(solution)/shard_map/ppermute | solution.py:50
  73.0 63.5 %collective-permute-start.12 = (bf16[2,640,384]{2,1,0:T(8,128)(2,1)S(1)}, bf16[2,640,384]{2,1,0:T(8,128)(2,1)S(1)}, u32[]{:S(2)}, u32[]{:S(2)}) collective-permute-start(bf16[2,640,384]{2,1,0:T(8,128)(2,1)S(1)} %collective-permute-done.10.refs_0_), channel_id=1, source_target_pairs={{0,32},{1,33},{2,34},{3,35},{4,36},{5,37},{6,38},{7,39},{8,40},{9,... | collective-permute-start | bytes 2949128 | tf_op jit(solution)/shard_map/ppermute | solution.py:50
  74.9 61.6 %copy-start.1 = (bf16[2,640,384]{2,1,0:T(8,128)(2,1)}, bf16[2,640,384]{2,1,0:T(8,128)(2,1)S(1)}, u32[]{:S(2)}) copy-start(bf16[2,640,384]{2,1,0:T(8,128)(2,1)S(1)} %collective-permute-done.11.refs_1_) | copy-start | bytes 2949124
  74.9 61.6 %collective-permute-start.13 = (bf16[2,640,384]{2,1,0:T(8,128)(2,1)S(1)}, bf16[2,640,384]{2,1,0:T(8,128)(2,1)}, u32[]{:S(2)}, u32[]{:S(2)}) collective-permute-start(bf16[2,640,384]{2,1,0:T(8,128)(2,1)S(1)} %collective-permute-done.11.refs_1_), channel_id=1, source_target_pairs={{0,32},{1,33},{2,34},{3,35},{4,36},{5,37},{6,38},{7,39},{8,40},{9,... | collective-permute-start | bytes 2949128 | tf_op jit(solution)/shard_map/ppermute | solution.py:50
  77.3 36.1 %collective-permute-start.15 = (bf16[384,640]{1,0:T(8,128)(2,1)}, bf16[384,640]{1,0:T(8,128)(2,1)}, u32[]{:S(2)}, u32[]{:S(2)}) collective-permute-start(bf16[384,640]{1,0:T(8,128)(2,1)} %collective-permute-done.14.refs_0_), channel_id=1, source_target_pairs={{0,256},{1,257},{2,258},{3,259},{4,260},{5,261},{6,262},{7,263},{8... | collective-permute-start | bytes 1474568 | tf_op jit(solution)/shard_map/ppermute | solution.py:50
  79.5 51.8 %copy-start.11 = (bf16[40,2560]{1,0:T(8,128)(2,1)}, bf16[40,2560]{1,0:T(8,128)(2,1)S(1)}, u32[]{:S(2)}) copy-start(bf16[40,2560]{1,0:T(8,128)(2,1)S(1)} %collective-permute-done.2.refs_0_.refs_4_) | copy-start | bytes 614404
  79.5 14.4 %collective-permute-start.4 = (bf16[40,2560]{1,0:T(8,128)(2,1)}, bf16[40,2560]{1,0:T(8,128)(2,1)}, u32[]{:S(2)}, u32[]{:S(2)}) collective-permute-start(bf16[40,2560]{1,0:T(8,128)(2,1)} %get-tuple-element.27), channel_id=1, source_target_pairs={{0,15},{1,14},{2,13},{3,12},{4,19},{5,18},{6,17},{7,16},{8,23},{9,... | collective-permute-start | bytes 614408 | tf_op jit(solution)/shard_map/ppermute | solution.py:50
  84.8 46.5 %copy-start.12 = (bf16[40,2560]{1,0:T(8,128)(2,1)}, bf16[40,2560]{1,0:T(8,128)(2,1)S(1)}, u32[]{:S(2)}) copy-start(bf16[40,2560]{1,0:T(8,128)(2,1)S(1)} %collective-permute-done.3.refs_1_.refs_5_) | copy-start | bytes 614404
  84.9 13.3 %collective-permute-start.5 = (bf16[40,2560]{1,0:T(8,128)(2,1)}, bf16[40,2560]{1,0:T(8,128)(2,1)}, u32[]{:S(2)}, u32[]{:S(2)}) collective-permute-start(bf16[40,2560]{1,0:T(8,128)(2,1)} %get-tuple-element.28), channel_id=1, source_target_pairs={{0,8},{1,9},{2,10},{3,11},{4,12},{5,13},{6,14},{7,15},{8,16},{9,17... | collective-permute-start | bytes 614408 | tf_op jit(solution)/shard_map/ppermute | solution.py:50
  93.9 12.3 %collective-permute-start.6 = (bf16[40,2560]{1,0:T(8,128)(2,1)}, bf16[40,2560]{1,0:T(8,128)(2,1)}, u32[]{:S(2)}, u32[]{:S(2)}) collective-permute-start(bf16[40,2560]{1,0:T(8,128)(2,1)} %get-tuple-element.29), channel_id=1, source_target_pairs={{0,11},{1,10},{2,9},{3,8},{4,15},{5,14},{6,13},{7,12},{8,19},{9,18... | collective-permute-start | bytes 614408 | tf_op jit(solution)/shard_map/ppermute | solution.py:50
  98.2 17.1 %collective-permute-start.7 = (bf16[40,2560]{1,0:T(8,128)(2,1)}, bf16[40,2560]{1,0:T(8,128)(2,1)}, u32[]{:S(2)}, u32[]{:S(2)}) collective-permute-start(bf16[40,2560]{1,0:T(8,128)(2,1)} %get-tuple-element.30), channel_id=1, source_target_pairs={{0,4},{1,5},{2,6},{3,7},{4,8},{5,9},{6,10},{7,11},{8,12},{9,13},{1... | collective-permute-start | bytes 614408 | tf_op jit(solution)/shard_map/ppermute | solution.py:50
  106.3 36.6 %collective-permute-start.16 = (bf16[384,640]{1,0:T(8,128)(2,1)}, bf16[384,640]{1,0:T(8,128)(2,1)}, u32[]{:S(2)}, u32[]{:S(2)}) collective-permute-start(bf16[384,640]{1,0:T(8,128)(2,1)} %collective-permute-done.14.refs_0_), channel_id=1, source_target_pairs={{0,32},{1,33},{2,34},{3,35},{4,36},{5,37},{6,38},{7,39},{8,40},{9,... | collective-permute-start | bytes 1474568 | tf_op jit(solution)/shard_map/ppermute | solution.py:50
  113.4 29.4 %collective-permute-start.17 = (bf16[384,640]{1,0:T(8,128)(2,1)}, bf16[384,640]{1,0:T(8,128)(2,1)}, u32[]{:S(2)}, u32[]{:S(2)}) collective-permute-start(bf16[384,640]{1,0:T(8,128)(2,1)} %collective-permute-done.15.refs_1_), channel_id=1, source_target_pairs={{0,32},{1,33},{2,34},{3,35},{4,36},{5,37},{6,38},{7,39},{8,40},{9,... | collective-permute-start | bytes 1474568 | tf_op jit(solution)/shard_map/ppermute | solution.py:50
  115.3 8.0 %collective-permute-start.8 = (bf16[40,2560]{1,0:T(8,128)(2,1)}, bf16[40,2560]{1,0:T(8,128)(2,1)}, u32[]{:S(2)}, u32[]{:S(2)}) collective-permute-start(bf16[40,2560]{1,0:T(8,128)(2,1)} %get-tuple-element.31), channel_id=1, source_target_pairs={{0,7},{1,6},{2,5},{3,4},{4,11},{5,10},{6,9},{7,8},{8,15},{9,14},{1... | collective-permute-start | bytes 614408 | tf_op jit(solution)/shard_map/ppermute | solution.py:50
  123.3 8.0 %collective-permute-start.9 = (bf16[40,2560]{1,0:T(8,128)(2,1)}, bf16[40,2560]{1,0:T(8,128)(2,1)}, u32[]{:S(2)}, u32[]{:S(2)}) collective-permute-start(bf16[40,2560]{1,0:T(8,128)(2,1)} %get-tuple-element.32), channel_id=1, source_target_pairs={{0,0},{1,1},{2,2},{3,3},{4,4},{5,5},{6,6},{7,7},{8,8},{9,9},{10,10... | collective-permute-start | bytes 614408 | tf_op jit(solution)/shard_map/ppermute | solution.py:50
  136.5 1.0 copy-start.2
  148.3 20.9 %collective-permute-start.18 = (bf16[40,2560]{1,0:T(8,128)(2,1)}, bf16[40,2560]{1,0:T(8,128)(2,1)S(1)}, u32[]{:S(2)}, u32[]{:S(2)}) collective-permute-start(bf16[40,2560]{1,0:T(8,128)(2,1)} %get-tuple-element.33), channel_id=1, source_target_pairs={{0,208},{1,209},{2,210},{3,211},{4,212},{5,213},{6,214},{7,215},{8... | collective-permute-start | bytes 614408 | tf_op jit(solution)/shard_map/ppermute | solution.py:50
  153.0 21.5 %collective-permute-start.19 = (bf16[40,2560]{1,0:T(8,128)(2,1)}, bf16[40,2560]{1,0:T(8,128)(2,1)S(1)}, u32[]{:S(2)}, u32[]{:S(2)}) collective-permute-start(bf16[40,2560]{1,0:T(8,128)(2,1)} %get-tuple-element.34), channel_id=1, source_target_pairs={{0,212},{1,213},{2,214},{3,215},{4,216},{5,217},{6,218},{7,219},{8... | collective-permute-start | bytes 614408 | tf_op jit(solution)/shard_map/ppermute | solution.py:50
  157.9 22.1 %collective-permute-start.20 = (bf16[40,2560]{1,0:T(8,128)(2,1)}, bf16[40,2560]{1,0:T(8,128)(2,1)S(1)}, u32[]{:S(2)}, u32[]{:S(2)}) collective-permute-start(bf16[40,2560]{1,0:T(8,128)(2,1)} %get-tuple-element.35), channel_id=1, source_target_pairs={{0,215},{1,214},{2,213},{3,212},{4,219},{5,218},{6,217},{7,216},{8... | collective-permute-start | bytes 614408 | tf_op jit(solution)/shard_map/ppermute | solution.py:50
  161.3 22.8 %collective-permute-start.21 = (bf16[40,2560]{1,0:T(8,128)(2,1)}, bf16[40,2560]{1,0:T(8,128)(2,1)S(1)}, u32[]{:S(2)}, u32[]{:S(2)}) collective-permute-start(bf16[40,2560]{1,0:T(8,128)(2,1)} %get-tuple-element.36), channel_id=1, source_target_pairs={{0,216},{1,217},{2,218},{3,219},{4,220},{5,221},{6,222},{7,223},{8... | collective-permute-start | bytes 614408 | tf_op jit(solution)/shard_map/ppermute | solution.py:50
  166.2 19.6 %collective-permute-start.22 = (bf16[40,2560]{1,0:T(8,128)(2,1)}, bf16[40,2560]{1,0:T(8,128)(2,1)S(1)}, u32[]{:S(2)}, u32[]{:S(2)}) collective-permute-start(bf16[40,2560]{1,0:T(8,128)(2,1)} %get-tuple-element.37), channel_id=1, source_target_pairs={{0,219},{1,218},{2,217},{3,216},{4,223},{5,222},{6,221},{7,220},{8... | collective-permute-start | bytes 614408 | tf_op jit(solution)/shard_map/ppermute | solution.py:50
  169.2 23.1 %copy-start.3 = (bf16[40,2560]{1,0:T(8,128)(2,1)}, bf16[40,2560]{1,0:T(8,128)(2,1)S(1)}, u32[]{:S(2)}) copy-start(bf16[40,2560]{1,0:T(8,128)(2,1)S(1)} %collective-permute-done.18.refs_0_) | copy-start | bytes 614404
  169.2 22.3 %collective-permute-start.23 = (bf16[40,2560]{1,0:T(8,128)(2,1)}, bf16[40,2560]{1,0:T(8,128)(2,1)S(1)}, u32[]{:S(2)}, u32[]{:S(2)}) collective-permute-start(bf16[40,2560]{1,0:T(8,128)(2,1)} %get-tuple-element.38), channel_id=1, source_target_pairs={{0,220},{1,221},{2,222},{3,223},{4,0},{5,1},{6,2},{7,3},{8,4},{9,5... | collective-permute-start | bytes 614408 | tf_op jit(solution)/shard_map/ppermute | solution.py:50
  174.5 17.8 %copy-start.4 = (bf16[40,2560]{1,0:T(8,128)(2,1)}, bf16[40,2560]{1,0:T(8,128)(2,1)S(1)}, u32[]{:S(2)}) copy-start(bf16[40,2560]{1,0:T(8,128)(2,1)S(1)} %collective-permute-done.19.refs_1_) | copy-start | bytes 614404
  174.5 17.0 %collective-permute-start.24 = (bf16[40,2560]{1,0:T(8,128)(2,1)}, bf16[40,2560]{1,0:T(8,128)(2,1)S(1)}, u32[]{:S(2)}, u32[]{:S(2)}) collective-permute-start(bf16[40,2560]{1,0:T(8,128)(2,1)} %get-tuple-element.39), channel_id=1, source_target_pairs={{0,223},{1,222},{2,221},{3,220},{4,3},{5,2},{6,1},{7,0},{8,7},{9,6... | collective-permute-start | bytes 614408 | tf_op jit(solution)/shard_map/ppermute | solution.py:50
  180.0 12.3 %copy-start.5 = (bf16[40,2560]{1,0:T(8,128)(2,1)}, bf16[40,2560]{1,0:T(8,128)(2,1)S(1)}, u32[]{:S(2)}) copy-start(bf16[40,2560]{1,0:T(8,128)(2,1)S(1)} %collective-permute-done.20.refs_2_) | copy-start | bytes 614404
  180.0 12.3 %collective-permute-start.25 = (bf16[40,2560]{1,0:T(8,128)(2,1)}, bf16[40,2560]{1,0:T(8,128)(2,1)S(1)}, u32[]{:S(2)}, u32[]{:S(2)}) collective-permute-start(bf16[40,2560]{1,0:T(8,128)(2,1)} %get-tuple-element.40), channel_id=1, source_target_pairs={{0,0},{1,1},{2,2},{3,3},{4,4},{5,5},{6,6},{7,7},{8,8},{9,9},{10,10... | collective-permute-start | bytes 614408 | tf_op jit(solution)/shard_map/ppermute | solution.py:50
  184.1 8.2 %copy-start.6 = (bf16[40,2560]{1,0:T(8,128)(2,1)}, bf16[40,2560]{1,0:T(8,128)(2,1)S(1)}, u32[]{:S(2)}) copy-start(bf16[40,2560]{1,0:T(8,128)(2,1)S(1)} %collective-permute-done.21.refs_3_) | copy-start | bytes 614404
  185.8 6.6 %copy-start.7 = (bf16[40,2560]{1,0:T(8,128)(2,1)}, bf16[40,2560]{1,0:T(8,128)(2,1)S(1)}, u32[]{:S(2)}) copy-start(bf16[40,2560]{1,0:T(8,128)(2,1)S(1)} %collective-permute-done.22.refs_4_) | copy-start | bytes 614404
  191.6 0.7 copy-start.8
  191.6 0.8 copy-start.9
  192.3 0.7 copy-start.10
  196.3 5.5 %collective-permute-start.26 = (bf16[128,2560]{1,0:T(8,128)(2,1)}, bf16[128,2560]{1,0:T(8,128)(2,1)S(1)}, u32[]{:S(2)}, u32[]{:S(2)}) collective-permute-start(bf16[128,2560]{1,0:T(8,128)(2,1)} %shard_map.101), channel_id=1, source_target_pairs={{0,32},{1,33},{2,34},{3,35},{4,36},{5,37},{6,38},{7,39},{8,40},{9,... | collective-permute-start | bytes 1966088 | tf_op jit(solution)/shard_map/ppermute | solution.py:50
